TPU v7x, 32 devices: a whole 2x2x4 slice. The times are simulated.
32 devices in a mesh: blk: 16 (over z, y, x), grp: 2 (over core).
Axes of the slice: x: 2, y: 2, z: 4, core: 2. Of those that a mesh axis runs over, the one named last changes fastest.
Arguments:
- returns: float32 [512, 8192], P(None, ('blk', 'grp')), may hold values from -200 to 200
Outputs:
- correlation: bfloat16 [8192, 8192], P(('blk', 'grp'))
All inputs are finite; a program needn't handle non-finite values.
Results may differ from a plain program's by a relative error of at most 0.0034.
Values may be sent and summed in bfloat16 or wider, within the bound.
A program may use at most 128 MiB of HBM per device.

v0:
```python
import math
import jax
import jax.numpy as jnp
from jax import lax
from jax.sharding import PartitionSpec as P


def gram_tile(first, second):
    return lax.dot_general(
        first, second, (((0,), (0,)), ((), ())), preferred_element_type=jnp.float32
    )


def shards(returns):
    bar_count = returns.shape[0]
    series_dev = returns.shape[1]
    devices = lax.axis_size(("blk", "grp"))
    my_index = lax.axis_index(("blk", "grp"))
    summed = lax.psum(jnp.sum(returns, axis=1), ("blk", "grp"))
    market = summed / (series_dev * devices)
    excess = returns - market[:, None]
    deviation = excess - jnp.mean(excess, axis=0, keepdims=True)
    inverse = lax.rsqrt(jnp.mean(deviation * deviation, axis=0, keepdims=True) + 1e-06) / math.sqrt(
        bar_count
    )
    zscores = (deviation * inverse).astype(jnp.bfloat16)
    piece = lax.all_gather(zscores, ("blk", "grp"), axis=1, tiled=True)
    products = gram_tile(zscores, piece)
    column_block = jnp.arange(piece.shape[1], dtype=jnp.int32) // series_dev
    return jnp.where(column_block[None, :] >= my_index, products, jnp.float32(0.0)).astype(
        jnp.bfloat16
    )


def solution(mesh):
    in_specs = (P(None, ("blk", "grp")),)
    out_specs = P(("blk", "grp"), None)
    return jax.shard_map(shards, mesh=mesh, in_specs=in_specs, out_specs=out_specs, check_vma=False)
```

profile of v0, /device:TPU:0, one launch (start us, length us, event | category | flops | bytes accessed | tf_op | source)
XLA Modules:
  0.0 158.5 jit_solution(11532635164527842564)
XLA Ops:
  6.5 0.0 all-gather.2.cloned.1.call-start
  6.5 1.2 reduce_sum.27
  7.7 42.0 %psum.7 = f32[512]{0:T(512)S(1)} all-reduce(f32[512]{0:T(512)S(1)} %reduce_sum.27), channel_id=1, replica_groups=mesh['blk'=16,'grp'=2] {'blk','grp'}, use_global_device_ids=true, to_apply=%region_1.0 | all-reduce | flops 512 | bytes 4096 | tf_op jit(solution)/shard_map/psum | solution.py:19
  49.7 1.2 subtract_reduce_fusion
  50.9 1.2 multiply_reduce_fusion
  52.1 1.9 %multiply_convert_fusion = bf16[512,256]{1,0:T(8,128)(2,1)} fusion(f32[512,256]{1,0:T(8,128)} %param.1, f32[256]{0:T(256)S(1)} %rsqrt_multiply_fusion, f32[256]{0:T(256)S(1)} %broadcast_multiply_fusion.1, f32[512]{0:T(512)S(1)} %broadcast_multiply_fusion), kind=kLoop, calls=%fused_computation.2 | loop fusion | flops 524288 | bytes 790528 | tf_op jit(solution)/shard_map/convert_element_type | solution.py:26
  54.0 0.0 all-gather.2.cloned.1.call-update
  54.1 89.7 %all-gather.2.cloned.1.call-done = bf16[512,8192]{1,0:T(8,128)(2,1)} async-done(((bf16[512,256]{1,0:T(8,128)(2,1)}), bf16[512,8192]{1,0:T(8,128)(2,1)}) %all-gather.2.cloned.1.call-update) | async-done | bytes 8388624 | tf_op jit(solution)/shard_map/all_gather | solution.py:27
  143.7 7.9 %fusion = bf16[256,8192]{1,0:T(8,128)(2,1)} fusion(bf16[512,256]{1,0:T(8,128)(2,1)} %multiply_convert_fusion, bf16[512,8192]{1,0:T(8,128)(2,1)} %all-gather.2.cloned.1.call-done, pred[8192]{0:T(1024)(128)(4,1)S(1)} %fusion.1), kind=kOutput, calls=%fused_computation.1 | convolution fusion | flops 2151677952 | bytes 12853248 | tf_op jit(solution)/shard_map/dot_general | solution.py:9
  (4 shorter events, 0.0 us)
Async XLA Ops:
  6.5 137.2 %all-gather.2.cloned.1.call-start = ((), (), s32[]{:S(2)}) async-start(), calls=%async_computation | async-start | bytes 8650752 | tf_op jit(solution)/shard_map/all_gather | solution.py:27
Sparse Core Ops, SparseCore 0:
  54.2 89.5 all-gather.1
where the time goes:
time: 159 us; the launch traced here: 158 us
  waiting for transfers between devices  89.7 us (56%)
  blocking collectives  42 us (26%)
  between operations  13.4 us (8%)
  matrix products  7.89 us (5%)
  other arithmetic  5.49 us (3%)
    all_gather x1, waiting for transfers between devices, shards(): piece = lax.all_gather(zscores, ('blk', 'grp'), axis=1, tiled=True)  89.7 us
    psum x1, blocking collectives, shards(): summed = lax.psum(jnp.sum(returns, axis=1), ('blk', 'grp'))  42 us
    dot_general x1, matrix products, gram_tile(): lax.dot_general(first, second, (((0,), (0,)), ((), ())), preferred_elemen...  7.89 us
  transfers between devices with their start and end apart: 1, of which 1 were waited for; matrix products, arithmetic and copies ran while one was open for 0% of the time, Pallas kernels for 0%

commit v1 on v0

--- a/solution.py
+++ b/solution.py
@@ -3,6 +3,7 @@
 import jax.numpy as jnp
 from jax import lax
 from jax.sharding import PartitionSpec as P
+from jax.lax import psum
 
 
 def gram_tile(first, second):
@@ -16,7 +17,9 @@
     series_dev = returns.shape[1]
     devices = lax.axis_size(("blk", "grp"))
     my_index = lax.axis_index(("blk", "grp"))
-    summed = lax.psum(jnp.sum(returns, axis=1), ("blk", "grp"))
+    inp = jnp.sum(returns, axis=1)
+    y2 = psum(inp, "grp")
+    summed = psum(y2, "blk")
     market = summed / (series_dev * devices)
     excess = returns - market[:, None]
     deviation = excess - jnp.mean(excess, axis=0, keepdims=True)

time: 159 us -> 159 us (level)
  blocking collectives: 42 us -> 46 us
  waiting for transfers between devices: 89.7 us -> 85.7 us
    psum x1 -> x2, blocking collectives: 42 us -> 46 us  [the longest x1 43.3 us: shards(): summed = psum(y2, 'blk')]
    all_gather x1, waiting for transfers between devices: 89.7 us -> 85.7 us  [shards(): piece = lax.all_gather(zscores, ('blk', 'grp'), axis=1, tiled=True)]
where the time goes in v1:
time: 159 us
  waiting for transfers between devices  85.7 us (54%)
  blocking collectives  46 us (29%)
  between operations  13.4 us (8%)
  matrix products  7.89 us (5%)
  other arithmetic  5.5 us (3%)
    all_gather x1, waiting for transfers between devices, shards(): piece = lax.all_gather(zscores, ('blk', 'grp'), axis=1, tiled=True)  85.7 us
    psum x1, blocking collectives, shards(): summed = psum(y2, 'blk')  43.3 us
    dot_general x1, matrix products, gram_tile(): lax.dot_general(first, second, (((0,), (0,)), ((), ())), preferred_elemen...  7.89 us
  transfers between devices with their start and end apart: 1, of which 1 were waited for; matrix products, arithmetic and copies ran while one was open for 0% of the time, Pallas kernels for 0%

profile of v1, /device:TPU:0, one launch (start us, length us, event | category | flops | bytes accessed | tf_op | source)
XLA Modules:
  0.0 158.5 jit_solution(8566085006919442909)
XLA Ops:
  6.5 0.0 all-gather.2.cloned.1.call-start
  6.5 1.2 reduce_sum.27
  7.7 2.6 %psum.14 = f32[512]{0:T(512)S(1)} all-reduce(f32[512]{0:T(512)S(1)} %reduce_sum.27), channel_id=1, replica_groups=mesh['blk'=16,'grp'=2] {'grp'}, use_global_device_ids=true, to_apply=%region_1.0 | all-reduce | flops 512 | bytes 4096 | tf_op jit(solution)/shard_map/psum | solution.py:21
  10.4 43.3 %psum.15 = f32[512]{0:T(512)S(1)} all-reduce(f32[512]{0:T(512)S(1)} %psum.14), channel_id=1, replica_groups=mesh['blk'=16,'grp'=2] {'blk'}, use_global_device_ids=true, to_apply=%region_2.0 | all-reduce | flops 512 | bytes 4096 | tf_op jit(solution)/shard_map/psum | solution.py:22
  53.7 1.2 subtract_reduce_fusion
  54.9 1.2 multiply_reduce_fusion
  56.1 1.9 %multiply_convert_fusion = bf16[512,256]{1,0:T(8,128)(2,1)} fusion(f32[512,256]{1,0:T(8,128)} %param.1, f32[256]{0:T(256)S(1)} %rsqrt_multiply_fusion, f32[256]{0:T(256)S(1)} %broadcast_multiply_fusion.1, f32[512]{0:T(512)S(1)} %broadcast_multiply_fusion), kind=kLoop, calls=%fused_computation.2 | loop fusion | flops 524288 | bytes 790528 | tf_op jit(solution)/shard_map/convert_element_type | solution.py:29
  58.0 0.0 all-gather.2.cloned.1.call-update
  58.0 85.7 %all-gather.2.cloned.1.call-done = bf16[512,8192]{1,0:T(8,128)(2,1)} async-done(((bf16[512,256]{1,0:T(8,128)(2,1)}), bf16[512,8192]{1,0:T(8,128)(2,1)}) %all-gather.2.cloned.1.call-update) | async-done | bytes 8388624 | tf_op jit(solution)/shard_map/all_gather | solution.py:30
  143.8 7.9 %fusion = bf16[256,8192]{1,0:T(8,128)(2,1)} fusion(bf16[512,256]{1,0:T(8,128)(2,1)} %multiply_convert_fusion, bf16[512,8192]{1,0:T(8,128)(2,1)} %all-gather.2.cloned.1.call-done, pred[8192]{0:T(1024)(128)(4,1)S(1)} %fusion.1), kind=kOutput, calls=%fused_computation.1 | convolution fusion | flops 2151677952 | bytes 12853248 | tf_op jit(solution)/shard_map/dot_general | solution.py:10
  (4 shorter events, 0.0 us)
Async XLA Ops:
  6.5 137.2 %all-gather.2.cloned.1.call-start = ((), (), s32[]{:S(2)}) async-start(), calls=%async_computation | async-start | bytes 8650752 | tf_op jit(solution)/shard_map/all_gather | solution.py:30
Sparse Core Ops, SparseCore 0:
  58.1 85.5 all-gather.1
